TPU v7x, 32 devices: a whole 2x2x4 slice. The times are simulated.
32 devices in a mesh: tm: 8 (over y, x, core), freq: 4 (over z).
Axes of the slice: x: 2, y: 2, z: 4, core: 2. Of those that a mesh axis runs over, the one named last changes fastest.
Arguments:
- sfts: float32 [384, 2, 4096], P('tm', None, 'freq'), may hold values from -40 to 40
- detector_ids: int32 [384], replicated, may hold values from 0 to 2
- intersection: float32 [3, 3], replicated, may hold values from 0.3 to 1
- lags: int32 [12], replicated, may hold values from 1 to 16, as said below
- template_ids: int32 [4096, 2], P('tm'), may hold values from 0 to 63
Outputs:
- stat: float32 [4096, 4096], P('tm', 'freq')
Inputs may be any that keep to these rules, and one draw needn't show every extreme that they name: 12 distinct lags, one of them 16.
All inputs are finite; a program needn't handle non-finite values.
Results may differ from a plain program's by a relative error of at most 0.009.
Values may be sent and summed in bfloat16 or wider, within the bound.
A program may use at most 64 MiB of HBM per device.

v0:
```python
import functools
import math

import jax
import jax.numpy as jnp
import numpy as np
from jax import lax
from jax.experimental import pallas as pl
from jax.experimental.pallas import tpu as pltpu
from jax.sharding import PartitionSpec as P

NBIN = 4096
LAGMAX = 16
NGRID = 64
PERIOD = 283
PIECE = 256
CHUNK = 96
MESH = pl.DeviceIdType.MESH


def even_series(function, degree):
    nodes = np.cos(np.pi * (np.arange(64) + 0.5) / 64) * 0.125 + 0.125
    fit = np.polynomial.chebyshev.Chebyshev.fit(nodes, function(np.sqrt(nodes)), degree, domain=[0, 0.25])
    return [float(c) for c in fit.convert(kind=np.polynomial.Polynomial).coef]


SIN_SERIES = even_series(lambda y: np.sin(2 * np.pi * y) / y, 6)
COS_SERIES = even_series(lambda y: np.cos(2 * np.pi * y), 7)


def horner(series, z):
    value = jnp.full_like(z, series[-1])
    for coefficient in series[-2::-1]:
        value = value * z + coefficient
    return value


def turn_cos_sin(turns):
    y = turns - jnp.round(turns)
    z = y * y
    return horner(COS_SERIES, z), y * horner(SIN_SERIES, z)


def xor(index, bits):
    out = index
    bit = 1
    while bit <= bits:
        if bits & bit:
            out = out + bit - 2 * bit * ((index // bit) % 2)
        bit *= 2
    return out


def kernel(
    n, nf, scale,
    x_ref, det_ref, inter_ref, lag_ref, tid_ref, out_ref,
    buf, pbuf, rbuf, rcol, detcol, table, factors, white, pairs,
    bulk_send, bulk_recv, p_send, p_recv, r_send, r_recv,
):
    me = lax.axis_index("tm")
    mf = lax.axis_index("freq")
    span = x_ref.shape[0]
    rows = n * span
    nlag = lag_ref.shape[0]
    pieces = buf.shape[0]
    templ = tid_ref.shape[1]
    evens = [o for o in range(2, n, 2)]

    re = x_ref[:, 0, :]
    im = x_ref[:, 1, :]
    for p in range(pieces):
        cols = slice(p * PIECE, (p + 1) * PIECE)
        buf[p, me, 0] = re[:, cols].astype(jnp.bfloat16)
        buf[p, me, 1] = im[:, cols].astype(jnp.bfloat16)
    local = jnp.sum(re * re + im * im, axis=1, keepdims=True)
    eye = lax.broadcasted_iota(jnp.int32, (span, 128), 0) == lax.broadcasted_iota(jnp.int32, (span, 128), 1)
    local_row = jnp.sum(jnp.where(eye, local, 0.0), axis=0, keepdims=True)
    pbuf[0] = jnp.broadcast_to(local_row, (8, 128))

    barrier = pltpu.get_barrier_semaphore()
    for d in range(1, nf):
        pl.semaphore_signal(barrier, inc=1, device_id=(me, (mf + d) % nf), device_id_type=MESH)
    for o in range(1, n):
        pl.semaphore_signal(barrier, inc=1, device_id=(xor(me, o), mf), device_id_type=MESH)
    pl.semaphore_wait(barrier, nf - 1 + n - 1)

    def power_copy(d):
        return pltpu.make_async_remote_copy(
            src_ref=pbuf.at[0], dst_ref=pbuf.at[d], send_sem=p_send.at[d], recv_sem=p_recv.at[d],
            device_id=(me, (mf + d) % nf), device_id_type=MESH)

    def rate_copy(o):
        return pltpu.make_async_remote_copy(
            src_ref=rbuf.at[me], dst_ref=rbuf.at[me], send_sem=r_send.at[o], recv_sem=r_recv.at[o],
            device_id=(xor(me, o), mf), device_id_type=MESH)

    def own_copy(p, o):
        return pltpu.make_async_remote_copy(
            src_ref=buf.at[p, me], dst_ref=buf.at[p, me], send_sem=bulk_send.at[p, o], recv_sem=bulk_recv.at[p, o],
            device_id=(xor(me, o), mf), device_id_type=MESH)

    def pass_copy(p, o):
        block = xor(me, o)
        return pltpu.make_async_remote_copy(
            src_ref=buf.at[p, block], dst_ref=buf.at[p, block],
            send_sem=bulk_send.at[p, o + 1], recv_sem=bulk_recv.at[p, o + 1],
            device_id=(xor(me, 1), mf), device_id_type=MESH)

    def landed(p, o):
        block = xor(me, o)
        pltpu.make_async_remote_copy(
            src_ref=buf.at[p, block], dst_ref=buf.at[p, block],
            send_sem=bulk_send.at[p, o], recv_sem=bulk_recv.at[p, o],
            device_id=(xor(me, o), mf), device_id_type=MESH).wait_recv()

    for d in range(1, nf):
        power_copy(d).start()
    for p in range(pieces):
        for o in evens + [1]:
            own_copy(p, o).start()

    tail = rows + LAGMAX
    index = lax.broadcasted_iota(jnp.int32, (tail, 128), 0).astype(jnp.float32)
    position = index - PERIOD * jnp.floor((index + 0.5) * (1.0 / PERIOD))
    cos_i, sin_i = turn_cos_sin(position * (1.0 / PERIOD))
    for c in range(templ // 128):
        cols = slice(c * 128, (c + 1) * 128)
        cos_q, sin_q = turn_cos_sin(tid_ref[1:2, cols].astype(jnp.float32) * (1.0 / NGRID))
        amplitude = (8.0 + 4.0 * tid_ref[0:1, cols].astype(jnp.float32)) * (0.5 / math.pi)
        cos_t, sin_t = turn_cos_sin(amplitude * (sin_i * cos_q + cos_i * sin_q))
        table[0, c] = cos_t
        table[1, c] = sin_t

    square = lax.broadcasted_iota(jnp.int32, (128, 128), 0) == lax.broadcasted_iota(jnp.int32, (128, 128), 1)
    for c in range(rows // 128):
        ids = det_ref[c * 128:(c + 1) * 128].astype(jnp.float32)[None, :]
        column = jnp.sum(jnp.where(square, ids, 0.0), axis=1, keepdims=True)
        detcol[c * 128:(c + 1) * 128, :] = jnp.broadcast_to(column, (128, 128))
    detcol[rows:tail, :] = jnp.full((LAGMAX, 128), -1.0, jnp.float32)
    white[:, :, rows:tail, :] = jnp.zeros((2, PIECE // 128, LAGMAX, 128), jnp.float32)

    ndet = inter_ref.shape[0]
    block = 128

    def factor_step(l, carry):
        lag = lag_ref[l]
        for r in range(rows // block):
            here = slice(r * block, (r + 1) * block)
            there = pl.ds(r * block + lag, block)
            near = detcol[here, :]
            far = detcol[there, :]
            weight = jnp.zeros((block, 128), jnp.float32)
            for b in range(ndet):
                gain = jnp.zeros((block, 128), jnp.float32)
                for a in range(ndet):
                    gain = jnp.where(near == a, inter_ref[a, b], gain)
                weight = jnp.where(far == b, gain, weight)
            for c in range(templ // 128):
                cols = slice(c * 128, (c + 1) * 128)
                ci = table[0, c, here, :] * weight
                si = table[1, c, here, :] * weight
                cj = table[0, c, there, :]
                sj = table[1, c, there, :]
                cosine = (ci * cj + si * sj).T.astype(jnp.bfloat16)
                sine = (ci * sj - si * cj).T.astype(jnp.bfloat16)
                start = pl.multiple_of(2 * rows * l + r * block, 128)
                factors[cols, pl.ds(start, block)] = cosine
                factors[cols, pl.ds(start + rows, block)] = sine
        return carry

    def forward(p):
        for o in evens:
            landed(p, o)
            pass_copy(p, o).start()

    half = nlag // 2
    lax.fori_loop(0, half, factor_step, 0)
    for d in range(1, nf):
        power_copy(d).wait_recv()
    total = pbuf[0]
    for d in range(1, nf):
        total = total + pbuf[d]
    rbuf[me] = lax.rsqrt(total * (1.0 / NBIN) + 1e-06)

    for o in range(1, n):
        rate_copy(o).start()

    forward(0)
    lax.fori_loop(half, nlag, factor_step, 0)

    for o in range(1, n):
        rate_copy_in = pltpu.make_async_remote_copy(
            src_ref=rbuf.at[xor(me, o)], dst_ref=rbuf.at[xor(me, o)], send_sem=r_send.at[o], recv_sem=r_recv.at[o],
            device_id=(xor(me, o), mf), device_id_type=MESH)
        rate_copy_in.wait_recv()
    for g in range(n):
        column = jnp.sum(jnp.where(eye, rbuf[g, 0:1, :], 0.0), axis=1, keepdims=True)
        rcol[g * span:(g + 1) * span, :] = jnp.broadcast_to(column, (span, 128))

    def piece_step(p, carry):
        for o in range(1, n, 2):
            landed(p, o)

        @pl.when(p + 1 < pieces)
        def _():
            forward(p + 1)

        for g in range(n):
            here = slice(g * span, (g + 1) * span)
            rate = rcol[here, :]
            for c in range(2):
                for h in range(PIECE // 128):
                    white[c, h, here, :] = buf[p, g, c, :, h * 128:(h + 1) * 128].astype(jnp.float32) * rate

        def pair_step(l, inner):
            lag = lag_ref[l]
            for r in range(rows // CHUNK):
                here = slice(r * CHUNK, (r + 1) * CHUNK)
                there = pl.ds(r * CHUNK + lag, CHUNK)
                start = pl.multiple_of(2 * rows * l + r * CHUNK, 32)
                for h in range(PIECE // 128):
                    cols = slice(h * 128, (h + 1) * 128)
                    a = white[0, h, here, :]
                    b = white[1, h, here, :]
                    c = white[0, h, there, :]
                    d = white[1, h, there, :]
                    pairs[pl.ds(start, CHUNK), cols] = (a * c + b * d).astype(jnp.bfloat16)
                    pairs[pl.ds(start + rows, CHUNK), cols] = (a * d - b * c).astype(jnp.bfloat16)
            return inner

        lax.fori_loop(0, nlag, pair_step, 0)
        product = jnp.dot(factors[...], pairs[...], preferred_element_type=jnp.float32)
        out_ref[:, pl.ds(pl.multiple_of(p * PIECE, PIECE), PIECE)] = (product * scale).astype(out_ref.dtype)
        return carry

    lax.fori_loop(0, pieces, piece_step, 0)

    for d in range(1, nf):
        power_copy(d).wait_send()
    for o in range(1, n):
        rate_copy(o).wait_send()

    def drain(p, carry):
        for o in evens + [1]:
            own_copy(p, o).wait_send()
        for o in evens:
            pass_copy(p, o).wait_send()
        return carry

    lax.fori_loop(0, pieces, drain, 0)


def shards(n, nf, sfts, detector_ids, intersection, lags, template_ids):
    span, _, width = sfts.shape
    rows = detector_ids.shape[0]
    nlag = lags.shape[0]
    templ = template_ids.shape[0]
    pieces = width // PIECE
    vmem = pl.BlockSpec(memory_space=pltpu.VMEM)
    smem = pl.BlockSpec(memory_space=pltpu.SMEM)
    scale = 1.0 / math.sqrt(rows * nlag)
    stat = pl.pallas_call(
        functools.partial(kernel, n, nf, scale),
        out_shape=jax.ShapeDtypeStruct((templ, width), jnp.bfloat16),
        in_specs=[vmem, vmem, smem, smem, vmem],
        out_specs=vmem,
        scratch_shapes=[
            pltpu.VMEM((pieces, n, 2, span, PIECE), jnp.bfloat16),
            pltpu.VMEM((nf, 8, 128), jnp.float32),
            pltpu.VMEM((n, 8, 128), jnp.float32),
            pltpu.VMEM((rows, 128), jnp.float32),
            pltpu.VMEM((rows + LAGMAX, 128), jnp.float32),
            pltpu.VMEM((2, templ // 128, rows + LAGMAX, 128), jnp.float32),
            pltpu.VMEM((templ, 2 * rows * nlag), jnp.bfloat16),
            pltpu.VMEM((2, PIECE // 128, rows + LAGMAX, 128), jnp.float32),
            pltpu.VMEM((2 * rows * nlag, PIECE), jnp.bfloat16),
            pltpu.SemaphoreType.DMA((pieces, n)),
            pltpu.SemaphoreType.DMA((pieces, n)),
            pltpu.SemaphoreType.DMA((nf,)),
            pltpu.SemaphoreType.DMA((nf,)),
            pltpu.SemaphoreType.DMA((n,)),
            pltpu.SemaphoreType.DMA((n,)),
        ],
        compiler_params=pltpu.CompilerParams(
            collective_id=0, has_side_effects=True, vmem_limit_bytes=60 * 1024 * 1024
        ),
    )(sfts, detector_ids, intersection, lags, template_ids.T)
    return stat.astype(jnp.float32)


def solution(mesh):
    n, nf = mesh.shape["tm"], mesh.shape["freq"]
    in_specs = (P("tm", None, "freq"), P(), P(), P(), P("tm", None))
    return jax.shard_map(
        functools.partial(shards, n, nf), mesh=mesh, in_specs=in_specs, out_specs=P("tm", "freq"), check_vma=False
    )
```

profile of v0, /device:TPU:0, one launch (start us, length us, event | category | flops | bytes accessed | tf_op | source)
XLA Modules:
  0.0 41.3 jit_solution(15047596686049634571)
XLA Ops:
  0.0 38.5 %shard_map.55 = bf16[512,1024]{1,0:T(8,128)(2,1)} custom-call(f32[48,2,1024]{2,1,0:T(2,128)} %x_ref.1, s32[384]{0:T(512)} %det_ref.1, f32[3,3]{1,0:T(4,128)} %inter_ref.1, s32[12]{0:T(128)} %lag_ref.1, s32[2,512]{1,0:T(2,128)} %bitcast.1), custom_call_target="tpu_custom_call" | custom-call | tf_op jit(solution)/shard_map/pallas_call | solution.py:262
  38.5 2.8 %convert_element_type.3 = f32[512,1024]{1,0:T(8,128)} convert(bf16[512,1024]{1,0:T(8,128)(2,1)} %shard_map.55) | non-fusion elementwise | flops 524288 | bytes 3145728 | tf_op jit(solution)/shard_map/convert_element_type | solution.py:288
where the time goes:
time: 41.4 us; the launch traced here: 41.3 us
  Pallas kernels  38.5 us (93%)
  other arithmetic  2.79 us (7%)
    pallas_call x1, Pallas kernels, shards(): pl.pallas_call(functools.partial(kernel, n, nf, scale), out_shape=jax.Sha...  38.5 us
    convert_element_type x1, other arithmetic, shards(): return stat.astype(jnp.float32)  2.79 us

commit v1 on v0

v1 whole, which is shorter than its diff:
```python
import functools
import math

import jax
import jax.numpy as jnp
import numpy as np
from jax import lax
from jax.experimental import pallas as pl
from jax.experimental.pallas import tpu as pltpu
from jax.sharding import PartitionSpec as P

NBIN = 4096
LAGMAX = 16
NGRID = 64
PERIOD = 283
PIECE = 256
MESH = pl.DeviceIdType.MESH


def even_series(function, degree):
    nodes = np.cos(np.pi * (np.arange(64) + 0.5) / 64) * 0.125 + 0.125
    fit = np.polynomial.chebyshev.Chebyshev.fit(nodes, function(np.sqrt(nodes)), degree, domain=[0, 0.25])
    return [float(c) for c in fit.convert(kind=np.polynomial.Polynomial).coef]


COS_SERIES = even_series(lambda y: np.cos(2 * np.pi * y), 7)


def horner(series, z):
    value = jnp.full_like(z, series[-1])
    for coefficient in series[-2::-1]:
        value = value * z + coefficient
    return value


def turn_cos(turns):
    y = turns - jnp.round(turns)
    return horner(COS_SERIES, y * y)


def xor(index, bits):
    out = index
    bit = 1
    while bit <= bits:
        if bits & bit:
            out = out + bit - 2 * bit * ((index // bit) % 2)
        bit *= 2
    return out


def bessel(argument, count):
    turn = np.arange(1024) * (2 * np.pi / 1024)
    wave = np.exp(1j * argument[..., None] * np.sin(turn))
    return np.real(np.fft.fft(wave, axis=-1) / 1024)[..., :count]


def argument_of(lag):
    return (8.0 + 4.0 * np.arange(NGRID)) * 2.0 * np.sin(np.pi * lag / PERIOD)


def harmonic_rows(nlag):
    rows = []
    for k in range(nlag):
        values = np.abs(bessel(argument_of(LAGMAX - nlag + 1 + k), 256))
        last = int(np.nonzero(values.max(axis=0) > 1e-5)[0].max())
        rows.append(-(-(last + 1) // 16) * 16)
    return rows


def row_harmonics(count):
    r = np.arange(count)
    even_n, even_s = 2 * ((r + 1) // 2), ((r > 0) & (r % 2 == 0)).astype(int)
    odd_n, odd_s = 2 * (r // 2) + 1, r % 2
    return np.concatenate([even_n, odd_n]), np.concatenate([even_s, odd_s])


def bessel_table(count, scale):
    n, _ = row_harmonics(count)
    values = np.stack([bessel(argument_of(lag), 256) for lag in range(1, LAGMAX + 1)])
    sign = np.where(n == 0, 1.0, 2.0) * np.where((n // 2) % 2 == 0, 1.0, -1.0) * scale
    table = (values[:, :, n] * sign).transpose(0, 2, 1)
    high = table.astype(jnp.bfloat16)
    low = (table - high.astype(np.float64)).astype(jnp.bfloat16)
    return np.concatenate([high, low], axis=2)


def kernel(
    n, nf, heads,
    x_ref, det_ref, inter_ref, lag_ref, tid_ref, bess_ref, out_ref,
    buf, pbuf, rbuf, rows_ref, shifted, weights, base, basis, bess, wave, factors, white, pairs, series, table_sem,
    bulk_send, bulk_recv, p_send, p_recv, r_send, r_recv,
):
    me = lax.axis_index("tm")
    mf = lax.axis_index("freq")
    span = x_ref.shape[0]
    rows = n * span
    nlag = lag_ref.shape[0]
    pieces = buf.shape[0]
    templ = tid_ref.shape[1]
    width = rows_ref.shape[2]
    most = base.shape[1]
    evens = [o for o in range(2, n, 2)]
    starts = [2 * sum(heads[:k]) for k in range(nlag + 1)]
    total_rows = starts[-1]

    table_copy = pltpu.make_async_copy(bess_ref, bess, table_sem)
    table_copy.start()

    re = x_ref[:, 0, :]
    im = x_ref[:, 1, :]
    for p in range(pieces):
        cols = slice(p * PIECE, (p + 1) * PIECE)
        buf[p, me, 0] = re[:, cols].astype(jnp.bfloat16)
        buf[p, me, 1] = im[:, cols].astype(jnp.bfloat16)
    local = jnp.sum(re * re + im * im, axis=1, keepdims=True)
    eye = lax.broadcasted_iota(jnp.int32, (span, 128), 0) == lax.broadcasted_iota(jnp.int32, (span, 128), 1)
    local_row = jnp.sum(jnp.where(eye, local, 0.0), axis=0, keepdims=True)
    pbuf[0] = jnp.broadcast_to(local_row, (8, 128))

    barrier = pltpu.get_barrier_semaphore()
    for d in range(1, nf):
        pl.semaphore_signal(barrier, inc=1, device_id=(me, (mf + d) % nf), device_id_type=MESH)
    for o in range(1, n):
        pl.semaphore_signal(barrier, inc=1, device_id=(xor(me, o), mf), device_id_type=MESH)
    pl.semaphore_wait(barrier, nf - 1 + n - 1)

    def power_copy(d):
        return pltpu.make_async_remote_copy(
            src_ref=pbuf.at[0], dst_ref=pbuf.at[d], send_sem=p_send.at[d], recv_sem=p_recv.at[d],
            device_id=(me, (mf + d) % nf), device_id_type=MESH)

    def rate_copy(o):
        return pltpu.make_async_remote_copy(
            src_ref=rbuf.at[me], dst_ref=rbuf.at[me], send_sem=r_send.at[o], recv_sem=r_recv.at[o],
            device_id=(xor(me, o), mf), device_id_type=MESH)

    def own_copy(p, o):
        return pltpu.make_async_remote_copy(
            src_ref=buf.at[p, me], dst_ref=buf.at[p, me], send_sem=bulk_send.at[p, o], recv_sem=bulk_recv.at[p, o],
            device_id=(xor(me, o), mf), device_id_type=MESH)

    def pass_copy(p, o):
        block = xor(me, o)
        return pltpu.make_async_remote_copy(
            src_ref=buf.at[p, block], dst_ref=buf.at[p, block],
            send_sem=bulk_send.at[p, o + 1], recv_sem=bulk_recv.at[p, o + 1],
            device_id=(xor(me, 1), mf), device_id_type=MESH)

    def landed(p, o):
        block = xor(me, o)
        pltpu.make_async_remote_copy(
            src_ref=buf.at[p, block], dst_ref=buf.at[p, block],
            send_sem=bulk_send.at[p, o], recv_sem=bulk_recv.at[p, o],
            device_id=(xor(me, o), mf), device_id_type=MESH).wait_recv()

    for d in range(1, nf):
        power_copy(d).start()
    for p in range(pieces):
        for o in evens + [1]:
            own_copy(p, o).start()

    lag = [lag_ref[l] for l in range(nlag)]
    for turn in range(nlag):
        for l in range(turn % 2, nlag - 1, 2):
            lag[l], lag[l + 1] = jnp.minimum(lag[l], lag[l + 1]), jnp.maximum(lag[l], lag[l + 1])
    lag = [jnp.maximum(value, 1) for value in lag]

    def harmonics(count, lanes):
        r = lax.broadcasted_iota(jnp.int32, (count, lanes), 0)
        even_n = 2 * ((r + 1) // 2)
        even_s = jnp.where(r > 0, 1 - r % 2, 0)
        odd_n = 2 * (r // 2) + 1
        odd_s = r % 2
        return [(a.astype(jnp.float32), b.astype(jnp.float32)) for a, b in ((even_n, even_s), (odd_n, odd_s))]

    for c in range(rows // 128):
        index = (lax.broadcasted_iota(jnp.int32, (most, 128), 1) + c * 128).astype(jnp.float32)
        position = index - PERIOD * jnp.floor((index + 0.5) * (1.0 / PERIOD))
        for parity, (harmonic, quarter) in enumerate(harmonics(most, 128)):
            steps = harmonic * position
            steps = steps - PERIOD * jnp.floor((steps + 0.5) * (1.0 / PERIOD))
            base[parity, :, c * 128:(c + 1) * 128] = turn_cos(steps * (1.0 / PERIOD) - 0.25 * quarter)

    lane = lax.broadcasted_iota(jnp.int32, (1, 2 * NGRID), 1)
    level = (lane % NGRID).astype(jnp.float32)
    for k in range(nlag):
        for parity, (harmonic, quarter) in enumerate(harmonics(heads[k], 2 * NGRID)):
            turns = harmonic * (level * (1.0 / NGRID))
            turns = turns - jnp.round(turns)
            half = harmonic * lag[k].astype(jnp.float32) * (0.5 / PERIOD)
            half = half - jnp.round(half)
            value = turn_cos(turns + half + 0.25 * quarter)
            high = value.astype(jnp.bfloat16).astype(jnp.float32)
            start = starts[k] + parity * heads[k]
            wave[start:start + heads[k], :] = jnp.where(lane < NGRID, high, value - high).astype(jnp.bfloat16)

    rows_ref[0] = jnp.full((8, width), -1.0, jnp.float32)
    for c in range(rows // 128):
        ids = det_ref[c * 128:(c + 1) * 128].astype(jnp.float32)[None, :]
        rows_ref[0, :, c * 128:(c + 1) * 128] = jnp.broadcast_to(ids, (8, 128))
    det_row = rows_ref[0, 0:1, :]
    for v in range(1, LAGMAX + 1):
        shifted[v - 1:v, :] = pltpu.roll(det_row, width - v, 1)
    near = det_row[:, :rows]
    far = shifted[:, :rows]
    ndet = inter_ref.shape[0]
    gains = jnp.zeros((LAGMAX, rows), jnp.float32)
    for b in range(ndet):
        gain = jnp.zeros((1, rows), jnp.float32)
        for a in range(ndet):
            gain = jnp.where(near == a, inter_ref[a, b], gain)
        gains = jnp.where(far == b, gain, gains)
    weights[...] = gains

    for h in range(PIECE // 128):
        white[:, h, rows:rows + LAGMAX, :] = jnp.zeros((2, LAGMAX, 128), jnp.float32)

    def forward(p):
        for o in evens:
            landed(p, o)
            pass_copy(p, o).start()

    for d in range(1, nf):
        power_copy(d).wait_recv()
    total = pbuf[0]
    for d in range(1, nf):
        total = total + pbuf[d]
    rbuf[me] = lax.rsqrt(total * (1.0 / NBIN) + 1e-06)
    for o in range(1, n):
        rate_copy(o).start()

    table_copy.wait()
    for k in range(nlag):
        for parity in range(2):
            start = starts[k] + parity * heads[k]
            series[start:start + heads[k], 0:2 * NGRID] = bess[lag[k] - 1, parity * most:parity * most + heads[k], :]
    grid_row = lax.broadcasted_iota(jnp.int32, (2 * NGRID, templ), 0) % NGRID
    pick_amplitude = (grid_row == tid_ref[0:1, :]).astype(jnp.float32).T.astype(jnp.bfloat16)
    pick_phase = (grid_row == tid_ref[1:2, :]).astype(jnp.float32).T.astype(jnp.bfloat16)
    contract = (((1,), (1,)), ((), ()))
    step = 256
    for c in range(total_rows // step):
        here = slice(c * step, (c + 1) * step)
        bessel_part = lax.dot_general(
            pick_amplitude, series[here, 0:2 * NGRID], contract, preferred_element_type=jnp.float32)
        wave_part = lax.dot_general(pick_phase, wave[here, :], contract, preferred_element_type=jnp.float32)
        factors[:, here] = (bessel_part * wave_part).astype(jnp.bfloat16)

    forward(0)

    for o in range(1, n):
        pltpu.make_async_remote_copy(
            src_ref=rbuf.at[xor(me, o)], dst_ref=rbuf.at[xor(me, o)], send_sem=r_send.at[o], recv_sem=r_recv.at[o],
            device_id=(xor(me, o), mf), device_id_type=MESH).wait_recv()
    valid = lax.broadcasted_iota(jnp.int32, (1, width), 1) < span
    rate_row = jnp.zeros((1, width), jnp.float32)
    for g in range(n):
        part = jnp.concatenate([rbuf[g, 0:1, :], jnp.zeros((1, width - 128), jnp.float32)], axis=1)
        part = jnp.where(valid, part, 0.0)
        rate_row = rate_row + (pltpu.roll(part, g * span, 1) if g else part)
    for v in range(1, LAGMAX + 1):
        shifted[v - 1:v, :] = pltpu.roll(rate_row, width - v, 1)
    weights[...] = weights[...] * (rate_row[:, :rows] * shifted[:, :rows])
    for k in range(nlag):
        weight = weights[pl.ds(lag[k] - 1, 1), :]
        for parity in range(2):
            start = starts[k] + parity * heads[k]
            basis[start:start + heads[k], :] = (base[parity, :heads[k], :] * weight).astype(jnp.bfloat16)

    chunk = 48

    def piece_step(p, carry):
        for o in range(1, n, 2):
            landed(p, o)

        @pl.when(p + 1 < pieces)
        def _():
            forward(p + 1)

        for g in range(n):
            here = slice(g * span, (g + 1) * span)
            for c in range(2):
                for h in range(PIECE // 128):
                    white[c, h, here, :] = buf[p, g, c, :, h * 128:(h + 1) * 128].astype(jnp.float32)

        for k in range(nlag):
            for r in range(rows // chunk):
                here = slice(r * chunk, (r + 1) * chunk)
                there = pl.ds(r * chunk + lag[k], chunk)
                for h in range(PIECE // 128):
                    cols = slice(h * 128, (h + 1) * 128)
                    a = white[0, h, here, :]
                    b = white[1, h, here, :]
                    c = white[0, h, there, :]
                    d = white[1, h, there, :]
                    pairs[k % 2, 0, here, cols] = (a * c + b * d).astype(jnp.bfloat16)
                    pairs[k % 2, 1, here, cols] = (a * d - b * c).astype(jnp.bfloat16)
            for parity in range(2):
                start = starts[k] + parity * heads[k]
                series[start:start + heads[k], :] = jnp.dot(
                    basis[start:start + heads[k], :], pairs[k % 2, parity],
                    preferred_element_type=jnp.float32).astype(jnp.bfloat16)
        product = jnp.dot(factors[...], series[...], preferred_element_type=jnp.float32)
        out_ref[:, pl.ds(pl.multiple_of(p * PIECE, PIECE), PIECE)] = product.astype(out_ref.dtype)
        return carry

    lax.fori_loop(0, pieces, piece_step, 0)

    for d in range(1, nf):
        power_copy(d).wait_send()
    for o in range(1, n):
        rate_copy(o).wait_send()

    def drain(p, carry):
        for o in evens + [1]:
            own_copy(p, o).wait_send()
        for o in evens:
            pass_copy(p, o).wait_send()
        return carry

    lax.fori_loop(0, pieces, drain, 0)


def shards(n, nf, sfts, detector_ids, intersection, lags, template_ids):
    span, _, width = sfts.shape
    rows = detector_ids.shape[0]
    nlag = lags.shape[0]
    templ = template_ids.shape[0]
    pieces = width // PIECE
    heads = harmonic_rows(nlag)
    most = max(heads)
    total_rows = 2 * sum(heads)
    table = jnp.asarray(bessel_table(most, 1.0 / math.sqrt(rows * nlag)))
    lanes = rows + 128
    vmem = pl.BlockSpec(memory_space=pltpu.VMEM)
    smem = pl.BlockSpec(memory_space=pltpu.SMEM)
    stat = pl.pallas_call(
        functools.partial(kernel, n, nf, heads),
        out_shape=jax.ShapeDtypeStruct((templ, width), jnp.bfloat16),
        in_specs=[vmem, vmem, smem, smem, vmem, pl.BlockSpec(memory_space=pl.ANY)],
        out_specs=vmem,
        scratch_shapes=[
            pltpu.VMEM((pieces, n, 2, span, PIECE), jnp.bfloat16),
            pltpu.VMEM((nf, 8, 128), jnp.float32),
            pltpu.VMEM((n, 8, 128), jnp.float32),
            pltpu.VMEM((1, 8, lanes), jnp.float32),
            pltpu.VMEM((LAGMAX, lanes), jnp.float32),
            pltpu.VMEM((LAGMAX, rows), jnp.float32),
            pltpu.VMEM((2, most, rows), jnp.float32),
            pltpu.VMEM((total_rows, rows), jnp.bfloat16),
            pltpu.VMEM(table.shape, jnp.bfloat16),
            pltpu.VMEM((total_rows, 2 * NGRID), jnp.bfloat16),
            pltpu.VMEM((templ, total_rows), jnp.bfloat16),
            pltpu.VMEM((2, PIECE // 128, rows + LAGMAX, 128), jnp.float32),
            pltpu.VMEM((2, 2, rows, PIECE), jnp.bfloat16),
            pltpu.VMEM((total_rows, PIECE), jnp.bfloat16),
            pltpu.SemaphoreType.DMA(()),
            pltpu.SemaphoreType.DMA((pieces, n)),
            pltpu.SemaphoreType.DMA((pieces, n)),
            pltpu.SemaphoreType.DMA((nf,)),
            pltpu.SemaphoreType.DMA((nf,)),
            pltpu.SemaphoreType.DMA((n,)),
            pltpu.SemaphoreType.DMA((n,)),
        ],
        compiler_params=pltpu.CompilerParams(
            collective_id=0, has_side_effects=True, vmem_limit_bytes=60 * 1024 * 1024
        ),
    )(sfts, detector_ids, intersection, lags, template_ids.T, table)
    return stat.astype(jnp.float32)


def solution(mesh):
    n, nf = mesh.shape["tm"], mesh.shape["freq"]
    in_specs = (P("tm", None, "freq"), P(), P(), P(), P("tm", None))
    return jax.shard_map(
        functools.partial(shards, n, nf), mesh=mesh, in_specs=in_specs, out_specs=P("tm", "freq"), check_vma=False
    )
```

time: 41.4 us -> 36.2 us (0.87)
  Pallas kernels: 38.5 us -> 33.3 us
    pallas_call x1, Pallas kernels: 38.5 us -> 33.3 us  [shards(): pl.pallas_call(functools.partial(kernel, n, nf, heads), out_shape=jax.Sha...]
where the time goes in v1:
time: 36.2 us; the launch traced here: 36.1 us
  Pallas kernels  33.3 us (92%)
  other arithmetic  2.79 us (8%)
    pallas_call x1, Pallas kernels, shards(): pl.pallas_call(functools.partial(kernel, n, nf, heads), out_shape=jax.Sha...  33.3 us
    convert_element_type x1, other arithmetic, shards(): return stat.astype(jnp.float32)  2.79 us

profile of v1, /device:TPU:0, one launch (start us, length us, event | category | flops | bytes accessed | tf_op | source)
XLA Modules:
  0.0 36.1 jit_solution(14996295593586792738)
XLA Ops:
  0.0 33.3 %shard_map.64 = bf16[512,1024]{1,0:T(8,128)(2,1)} custom-call(f32[48,2,1024]{2,1,0:T(2,128)} %x_ref.1, s32[384]{0:T(512)} %det_ref.1, f32[3,3]{1,0:T(4,128)} %inter_ref.1, s32[12]{0:T(128)} %lag_ref.1, s32[2,512]{1,0:T(2,128)} %bitcast.1, bf16[16,224,128]{2,1,0:T(8,128)(2,1)} %constant.2.clone.bess_ref), custom_call_target="tpu_custom_call" | custom-call | tf_op jit(solution)/shard_map/pallas_call | solution.py:337
  33.3 2.8 %convert_element_type.3 = f32[512,1024]{1,0:T(8,128)} convert(bf16[512,1024]{1,0:T(8,128)(2,1)} %shard_map.64) | non-fusion elementwise | flops 524288 | bytes 3145728 | tf_op jit(solution)/shard_map/convert_element_type | solution.py:369

commit v2 on v1

--- a/solution.py
+++ b/solution.py
@@ -86,8 +86,9 @@
 
 def kernel(
     n, nf, heads,
-    x_ref, det_ref, inter_ref, lag_ref, tid_ref, bess_ref, out_ref,
-    buf, pbuf, rbuf, rows_ref, shifted, weights, base, basis, bess, wave, factors, white, pairs, series, table_sem,
+    x_hbm, det_hbm, inter_hbm, lag_hbm, tid_hbm, bess_hbm, out_ref,
+    x_ref, det_ref, inter_ref, lag_ref, tid_ref,
+    buf, pbuf, rows_ref, shifted, weights, base, basis, bess, wave, picked, factors, white, near_rows, series, load_sem,
     bulk_send, bulk_recv, p_send, p_recv, r_send, r_recv,
 ):
     me = lax.axis_index("tm")
@@ -99,40 +100,47 @@
     templ = tid_ref.shape[1]
     width = rows_ref.shape[2]
     most = base.shape[1]
-    evens = [o for o in range(2, n, 2)]
+    evens = sorted(range(2, n, 2), key=lambda o: -bin(o).count("1"))
     starts = [2 * sum(heads[:k]) for k in range(nlag + 1)]
     total_rows = starts[-1]
 
-    table_copy = pltpu.make_async_copy(bess_ref, bess, table_sem)
-    table_copy.start()
-
-    re = x_ref[:, 0, :]
-    im = x_ref[:, 1, :]
-    for p in range(pieces):
-        cols = slice(p * PIECE, (p + 1) * PIECE)
-        buf[p, me, 0] = re[:, cols].astype(jnp.bfloat16)
-        buf[p, me, 1] = im[:, cols].astype(jnp.bfloat16)
-    local = jnp.sum(re * re + im * im, axis=1, keepdims=True)
-    eye = lax.broadcasted_iota(jnp.int32, (span, 128), 0) == lax.broadcasted_iota(jnp.int32, (span, 128), 1)
-    local_row = jnp.sum(jnp.where(eye, local, 0.0), axis=0, keepdims=True)
-    pbuf[0] = jnp.broadcast_to(local_row, (8, 128))
-
+    loads = [
+        pltpu.make_async_copy(source, target, load_sem.at[i])
+        for i, (source, target) in enumerate([
+            (x_hbm, x_ref), (lag_hbm, lag_ref), (det_hbm, det_ref), (tid_hbm, tid_ref), (inter_hbm, inter_ref),
+            (bess_hbm, bess)])
+    ]
+    for load in loads:
+        load.start()
     barrier = pltpu.get_barrier_semaphore()
     for d in range(1, nf):
         pl.semaphore_signal(barrier, inc=1, device_id=(me, (mf + d) % nf), device_id_type=MESH)
     for o in range(1, n):
         pl.semaphore_signal(barrier, inc=1, device_id=(xor(me, o), mf), device_id_type=MESH)
+
+    loads[0].wait()
+    re = x_ref[:, 0, :]
+    im = x_ref[:, 1, :]
+    local = jnp.sum(re * re + im * im, axis=1, keepdims=True)
+    eye = lax.broadcasted_iota(jnp.int32, (span, 128), 0) == lax.broadcasted_iota(jnp.int32, (span, 128), 1)
+    pbuf[0, pl.ds(me, 1), :] = jnp.sum(jnp.where(eye, local, 0.0), axis=0, keepdims=True)
+    for p in range(pieces):
+        for h in range(PIECE // 128):
+            cols = slice(p * PIECE + h * 128, p * PIECE + (h + 1) * 128)
+            buf[p, me, 0, h] = re[:, cols].astype(jnp.bfloat16)
+            buf[p, me, 1, h] = im[:, cols].astype(jnp.bfloat16)
     pl.semaphore_wait(barrier, nf - 1 + n - 1)
+
+    def share_copy(o, block):
+        return pltpu.make_async_remote_copy(
+            src_ref=pbuf.at[0, pl.ds(block, 1)], dst_ref=pbuf.at[0, pl.ds(block, 1)],
+            send_sem=r_send.at[o], recv_sem=r_recv.at[o],
+            device_id=(xor(me, o), mf), device_id_type=MESH)
 
     def power_copy(d):
         return pltpu.make_async_remote_copy(
             src_ref=pbuf.at[0], dst_ref=pbuf.at[d], send_sem=p_send.at[d], recv_sem=p_recv.at[d],
             device_id=(me, (mf + d) % nf), device_id_type=MESH)
-
-    def rate_copy(o):
-        return pltpu.make_async_remote_copy(
-            src_ref=rbuf.at[me], dst_ref=rbuf.at[me], send_sem=r_send.at[o], recv_sem=r_recv.at[o],
-            device_id=(xor(me, o), mf), device_id_type=MESH)
 
     def own_copy(p, o):
         return pltpu.make_async_remote_copy(
@@ -153,12 +161,14 @@
             send_sem=bulk_send.at[p, o], recv_sem=bulk_recv.at[p, o],
             device_id=(xor(me, o), mf), device_id_type=MESH).wait_recv()
 
-    for d in range(1, nf):
-        power_copy(d).start()
+    for o in evens + [1] + list(range(3, n, 2)):
+        share_copy(o, me).start()
     for p in range(pieces):
         for o in evens + [1]:
             own_copy(p, o).start()
 
+    for load in loads[1:5]:
+        load.wait()
     lag = [lag_ref[l] for l in range(nlag)]
     for turn in range(nlag):
         for l in range(turn % 2, nlag - 1, 2):
@@ -216,24 +226,20 @@
         white[:, h, rows:rows + LAGMAX, :] = jnp.zeros((2, LAGMAX, 128), jnp.float32)
 
     def forward(p):
-        for o in evens:
+        for o in evens[::-1]:
             landed(p, o)
             pass_copy(p, o).start()
 
+    for o in range(1, n):
+        share_copy(o, xor(me, o)).wait_recv()
     for d in range(1, nf):
-        power_copy(d).wait_recv()
-    total = pbuf[0]
-    for d in range(1, nf):
-        total = total + pbuf[d]
-    rbuf[me] = lax.rsqrt(total * (1.0 / NBIN) + 1e-06)
-    for o in range(1, n):
-        rate_copy(o).start()
-
-    table_copy.wait()
+        power_copy(d).start()
+
+    loads[5].wait()
     for k in range(nlag):
         for parity in range(2):
             start = starts[k] + parity * heads[k]
-            series[start:start + heads[k], 0:2 * NGRID] = bess[lag[k] - 1, parity * most:parity * most + heads[k], :]
+            picked[start:start + heads[k], :] = bess[lag[k] - 1, parity * most:parity * most + heads[k], :]
     grid_row = lax.broadcasted_iota(jnp.int32, (2 * NGRID, templ), 0) % NGRID
     pick_amplitude = (grid_row == tid_ref[0:1, :]).astype(jnp.float32).T.astype(jnp.bfloat16)
     pick_phase = (grid_row == tid_ref[1:2, :]).astype(jnp.float32).T.astype(jnp.bfloat16)
@@ -242,22 +248,24 @@
     for c in range(total_rows // step):
         here = slice(c * step, (c + 1) * step)
         bessel_part = lax.dot_general(
-            pick_amplitude, series[here, 0:2 * NGRID], contract, preferred_element_type=jnp.float32)
+            pick_amplitude, picked[here, :], contract, preferred_element_type=jnp.float32)
         wave_part = lax.dot_general(pick_phase, wave[here, :], contract, preferred_element_type=jnp.float32)
-        factors[:, here] = (bessel_part * wave_part).astype(jnp.bfloat16)
+        product = bessel_part * wave_part
+        for h in range(step // 128):
+            factors[c * (step // 128) + h] = product[:, h * 128:(h + 1) * 128].astype(jnp.bfloat16)
 
     forward(0)
 
-    for o in range(1, n):
-        pltpu.make_async_remote_copy(
-            src_ref=rbuf.at[xor(me, o)], dst_ref=rbuf.at[xor(me, o)], send_sem=r_send.at[o], recv_sem=r_recv.at[o],
-            device_id=(xor(me, o), mf), device_id_type=MESH).wait_recv()
-    valid = lax.broadcasted_iota(jnp.int32, (1, width), 1) < span
-    rate_row = jnp.zeros((1, width), jnp.float32)
-    for g in range(n):
-        part = jnp.concatenate([rbuf[g, 0:1, :], jnp.zeros((1, width - 128), jnp.float32)], axis=1)
-        part = jnp.where(valid, part, 0.0)
-        rate_row = rate_row + (pltpu.roll(part, g * span, 1) if g else part)
+    total = pbuf[0]
+    for d in range(1, nf):
+        power_copy(d).wait_recv()
+        total = total + pbuf[d]
+    rates = lax.rsqrt(total * (1.0 / NBIN) + 1e-06)
+    rates = jnp.where(lax.broadcasted_iota(jnp.int32, (n, 128), 1) < span, rates, 0.0)
+    rates = jnp.concatenate([rates, jnp.zeros((n, width - 128), jnp.float32)], axis=1)
+    rate_row = rates[0:1]
+    for g in range(1, n):
+        rate_row = rate_row + pltpu.roll(rates[g:g + 1], g * span, 1)
     for v in range(1, LAGMAX + 1):
         shifted[v - 1:v, :] = pltpu.roll(rate_row, width - v, 1)
     weights[...] = weights[...] * (rate_row[:, :rows] * shifted[:, :rows])
@@ -265,42 +273,43 @@
         weight = weights[pl.ds(lag[k] - 1, 1), :]
         for parity in range(2):
             start = starts[k] + parity * heads[k]
-            basis[start:start + heads[k], :] = (base[parity, :heads[k], :] * weight).astype(jnp.bfloat16)
-
-    chunk = 48
+            for c in range(rows // 128):
+                cols = slice(c * 128, (c + 1) * 128)
+                basis[c, start:start + heads[k], :] = (base[parity, :heads[k], cols] * weight[:, cols]).astype(jnp.bfloat16)
 
     def piece_step(p, carry):
         for o in range(1, n, 2):
             landed(p, o)
-
-        @pl.when(p + 1 < pieces)
-        def _():
-            forward(p + 1)
 
         for g in range(n):
             here = slice(g * span, (g + 1) * span)
             for c in range(2):
                 for h in range(PIECE // 128):
-                    white[c, h, here, :] = buf[p, g, c, :, h * 128:(h + 1) * 128].astype(jnp.float32)
+                    white[c, h, here, :] = buf[p, g, c, h].astype(jnp.float32)
+                    near_rows[c, h, here, :] = buf[p, g, c, h]
 
         for k in range(nlag):
-            for r in range(rows // chunk):
-                here = slice(r * chunk, (r + 1) * chunk)
-                there = pl.ds(r * chunk + lag[k], chunk)
-                for h in range(PIECE // 128):
-                    cols = slice(h * 128, (h + 1) * 128)
-                    a = white[0, h, here, :]
-                    b = white[1, h, here, :]
-                    c = white[0, h, there, :]
-                    d = white[1, h, there, :]
-                    pairs[k % 2, 0, here, cols] = (a * c + b * d).astype(jnp.bfloat16)
-                    pairs[k % 2, 1, here, cols] = (a * d - b * c).astype(jnp.bfloat16)
+            if k == nlag // 2:
+                @pl.when(p + 1 < pieces)
+                def _():
+                    forward(p + 1)
+
+            there = pl.ds(lag[k], rows)
+            a, b = [jnp.concatenate([near_rows[part, h] for h in range(PIECE // 128)], axis=1) for part in range(2)]
+            c, d = [
+                jnp.concatenate([white[part, h, there, :] for h in range(PIECE // 128)], axis=1).astype(jnp.bfloat16)
+                for part in range(2)]
             for parity in range(2):
                 start = starts[k] + parity * heads[k]
-                series[start:start + heads[k], :] = jnp.dot(
-                    basis[start:start + heads[k], :], pairs[k % 2, parity],
-                    preferred_element_type=jnp.float32).astype(jnp.bfloat16)
-        product = jnp.dot(factors[...], series[...], preferred_element_type=jnp.float32)
+                both = a * d - b * c if parity else a * c + b * d
+                piece = jnp.dot(
+                    jnp.concatenate([basis[c, start:start + heads[k], :] for c in range(rows // 128)], axis=1),
+                    both, preferred_element_type=jnp.float32)
+                for h in range(PIECE // 128):
+                    series[h, start:start + heads[k], :] = piece[:, h * 128:(h + 1) * 128].astype(jnp.bfloat16)
+        product = jnp.dot(
+            jnp.concatenate([factors[c] for c in range(total_rows // 128)], axis=1),
+            jnp.concatenate([series[h] for h in range(PIECE // 128)], axis=1), preferred_element_type=jnp.float32)
         out_ref[:, pl.ds(pl.multiple_of(p * PIECE, PIECE), PIECE)] = product.astype(out_ref.dtype)
         return carry
 
@@ -309,7 +318,7 @@
     for d in range(1, nf):
         power_copy(d).wait_send()
     for o in range(1, n):
-        rate_copy(o).wait_send()
+        share_copy(o, me).wait_send()
 
     def drain(p, carry):
         for o in evens + [1]:
@@ -333,28 +342,36 @@
     table = jnp.asarray(bessel_table(most, 1.0 / math.sqrt(rows * nlag)))
     lanes = rows + 128
     vmem = pl.BlockSpec(memory_space=pltpu.VMEM)
-    smem = pl.BlockSpec(memory_space=pltpu.SMEM)
-    stat = pl.pallas_call(
+    operands = [
+        pltpu.with_memory_space_constraint(operand, pltpu.HBM)
+        for operand in (sfts, detector_ids, intersection, lags, template_ids.T, table)
+    ]
+    return pl.pallas_call(
         functools.partial(kernel, n, nf, heads),
-        out_shape=jax.ShapeDtypeStruct((templ, width), jnp.bfloat16),
-        in_specs=[vmem, vmem, smem, smem, vmem, pl.BlockSpec(memory_space=pl.ANY)],
+        out_shape=pltpu.VMEM((templ, width), jnp.float32),
+        in_specs=[pl.BlockSpec(memory_space=pltpu.HBM)] * 6,
         out_specs=vmem,
         scratch_shapes=[
-            pltpu.VMEM((pieces, n, 2, span, PIECE), jnp.bfloat16),
-            pltpu.VMEM((nf, 8, 128), jnp.float32),
-            pltpu.VMEM((n, 8, 128), jnp.float32),
+            pltpu.VMEM(sfts.shape, jnp.float32),
+            pltpu.VMEM((rows,), jnp.int32),
+            pltpu.SMEM(intersection.shape, jnp.float32),
+            pltpu.SMEM((nlag,), jnp.int32),
+            pltpu.VMEM((2, templ), jnp.int32),
+            pltpu.VMEM((pieces, n, 2, PIECE // 128, span, 128), jnp.bfloat16),
+            pltpu.VMEM((nf, n, 128), jnp.float32),
             pltpu.VMEM((1, 8, lanes), jnp.float32),
             pltpu.VMEM((LAGMAX, lanes), jnp.float32),
             pltpu.VMEM((LAGMAX, rows), jnp.float32),
             pltpu.VMEM((2, most, rows), jnp.float32),
-            pltpu.VMEM((total_rows, rows), jnp.bfloat16),
+            pltpu.VMEM((rows // 128, total_rows, 128), jnp.bfloat16),
             pltpu.VMEM(table.shape, jnp.bfloat16),
             pltpu.VMEM((total_rows, 2 * NGRID), jnp.bfloat16),
-            pltpu.VMEM((templ, total_rows), jnp.bfloat16),
+            pltpu.VMEM((total_rows, 2 * NGRID), jnp.bfloat16),
+            pltpu.VMEM((total_rows // 128, templ, 128), jnp.bfloat16),
             pltpu.VMEM((2, PIECE // 128, rows + LAGMAX, 128), jnp.float32),
-            pltpu.VMEM((2, 2, rows, PIECE), jnp.bfloat16),
-            pltpu.VMEM((total_rows, PIECE), jnp.bfloat16),
-            pltpu.SemaphoreType.DMA(()),
+            pltpu.VMEM((2, PIECE // 128, rows, 128), jnp.bfloat16),
+            pltpu.VMEM((PIECE // 128, total_rows, 128), jnp.bfloat16),
+            pltpu.SemaphoreType.DMA((6,)),
             pltpu.SemaphoreType.DMA((pieces, n)),
             pltpu.SemaphoreType.DMA((pieces, n)),
             pltpu.SemaphoreType.DMA((nf,)),
@@ -363,10 +380,9 @@
             pltpu.SemaphoreType.DMA((n,)),
         ],
         compiler_params=pltpu.CompilerParams(
-            collective_id=0, has_side_effects=True, vmem_limit_bytes=60 * 1024 * 1024
+            collective_id=0, has_side_effects=True, vmem_limit_bytes=48 * 1024 * 1024
         ),
-    )(sfts, detector_ids, intersection, lags, template_ids.T, table)
-    return stat.astype(jnp.float32)
+    )(*operands)
 
 
 def solution(mesh):

time: 36.2 us -> 23.5 us (0.65)
  Pallas kernels: 33.3 us -> 22.1 us
  other arithmetic: 2.79 us -> 0 us
  local copies, waits for them, and re-layouts: 0 us -> 1.32 us
    pallas_call x1, Pallas kernels: 33.3 us -> 22.1 us  [shards(): pl.pallas_call(functools.partial(kernel, n, nf, heads), out_shape=pltpu.V...]
    convert_element_type x1 -> x0, other arithmetic: 2.79 us -> none  [shards(): return stat.astype(jnp.float32)]
    unnamed x0 -> x1, local copies, waits for them, and re-layouts: none -> 1.32 us
where the time goes in v2:
time: 23.5 us; the launch traced here: 23.4 us
  Pallas kernels  22.1 us (94%)
  local copies, waits for them, and re-layouts  1.32 us (6%)
    pallas_call x1, Pallas kernels, shards(): pl.pallas_call(functools.partial(kernel, n, nf, heads), out_shape=pltpu.V...  22.1 us
    unnamed x1, local copies, waits for them, and re-layouts  1.32 us

profile of v2, /device:TPU:0, one launch (start us, length us, event | category | flops | bytes accessed | tf_op | source)
XLA Modules:
  0.0 23.4 jit_solution(556323370213462965)
XLA Ops:
  0.0 22.1 %shard_map.64 = f32[512,1024]{1,0:T(8,128)S(1)} custom-call(f32[48,2,1024]{2,1,0:T(2,128)} %x_hbm.1, s32[384]{0:T(512)} %det_hbm.1, f32[3,3]{1,0:T(4,128)} %inter_hbm.1, s32[12]{0:T(128)} %lag_hbm.1, s32[2,512]{1,0:T(2,128)} %bitcast.1, bf16[16,224,128]{2,1,0:T(8,128)(2,1)} %constant.2.clone.bess_hbm), custom_call_target="tpu_custom_call" | custom-call | tf_op jit(solution)/shard_map/pallas_call | solution.py:349
  22.1 1.3 %copy.8 = f32[512,1024]{1,0:T(8,128)} copy(f32[512,1024]{1,0:T(8,128)S(1)} %shard_map.64) | data formatting | bytes 4194304

commit v3 on v2

--- a/solution.py
+++ b/solution.py
@@ -288,25 +288,36 @@
                     white[c, h, here, :] = buf[p, g, c, h].astype(jnp.float32)
                     near_rows[c, h, here, :] = buf[p, g, c, h]
 
-        for k in range(nlag):
-            if k == nlag // 2:
+        for group in range(0, nlag, 1):
+            if group == 2:
                 @pl.when(p + 1 < pieces)
                 def _():
                     forward(p + 1)
 
-            there = pl.ds(lag[k], rows)
-            a, b = [jnp.concatenate([near_rows[part, h] for h in range(PIECE // 128)], axis=1) for part in range(2)]
-            c, d = [
-                jnp.concatenate([white[part, h, there, :] for h in range(PIECE // 128)], axis=1).astype(jnp.bfloat16)
-                for part in range(2)]
-            for parity in range(2):
-                start = starts[k] + parity * heads[k]
-                both = a * d - b * c if parity else a * c + b * d
-                piece = jnp.dot(
-                    jnp.concatenate([basis[c, start:start + heads[k], :] for c in range(rows // 128)], axis=1),
-                    both, preferred_element_type=jnp.float32)
-                for h in range(PIECE // 128):
-                    series[h, start:start + heads[k], :] = piece[:, h * 128:(h + 1) * 128].astype(jnp.bfloat16)
+            slots = range(group, group + 1)
+            sums = [[0.0, 0.0] for _ in slots]
+            for first, last in [(lo, min(lo + 256, rows)) for lo in range(0, rows, 256)]:
+                count = last - first
+                a, b = [
+                    jnp.concatenate([near_rows[part, h, first:last] for h in range(PIECE // 128)], axis=1)
+                    for part in range(2)]
+                for at, k in enumerate(slots):
+                    there = pl.ds(lag[k] + first, count)
+                    c, d = [
+                        jnp.concatenate([white[part, h, there, :] for h in range(PIECE // 128)], axis=1).astype(jnp.bfloat16)
+                        for part in range(2)]
+                    for parity in range(2):
+                        start = starts[k] + parity * heads[k]
+                        both = a * d - b * c if parity else a * c + b * d
+                        sums[at][parity] += jnp.dot(
+                            jnp.concatenate(
+                                [basis[t, start:start + heads[k], :] for t in range(first // 128, last // 128)], axis=1),
+                            both, preferred_element_type=jnp.float32)
+            for at, k in enumerate(slots):
+                for parity in range(2):
+                    start = starts[k] + parity * heads[k]
+                    for h in range(PIECE // 128):
+                        series[h, start:start + heads[k], :] = sums[at][parity][:, h * 128:(h + 1) * 128].astype(jnp.bfloat16)
         product = jnp.dot(
             jnp.concatenate([factors[c] for c in range(total_rows // 128)], axis=1),
             jnp.concatenate([series[h] for h in range(PIECE // 128)], axis=1), preferred_element_type=jnp.float32)
@@ -368,8 +379,8 @@
             pltpu.VMEM((total_rows, 2 * NGRID), jnp.bfloat16),
             pltpu.VMEM((total_rows, 2 * NGRID), jnp.bfloat16),
             pltpu.VMEM((total_rows // 128, templ, 128), jnp.bfloat16),
-            pltpu.VMEM((2, PIECE // 128, rows + LAGMAX, 128), jnp.float32),
-            pltpu.VMEM((2, PIECE // 128, rows, 128), jnp.bfloat16),
+            pltpu.VMEM((2, PIECE // 128, rows + LAGMAX + 8, 128), jnp.float32),
+            pltpu.VMEM((2, PIECE // 128, rows + 16, 128), jnp.bfloat16),
             pltpu.VMEM((PIECE // 128, total_rows, 128), jnp.bfloat16),
             pltpu.SemaphoreType.DMA((6,)),
             pltpu.SemaphoreType.DMA((pieces, n)),

time: 23.5 us -> 23 us (0.979)
  Pallas kernels: 22.1 us -> 21.5 us
    pallas_call x1, Pallas kernels: 22.1 us -> 21.5 us  [shards(): pl.pallas_call(functools.partial(kernel, n, nf, heads), out_shape=pltpu.V...]
where the time goes in v3:
time: 23 us; the launch traced here: 22.9 us
  Pallas kernels  21.5 us (93%)
  local copies, waits for them, and re-layouts  1.32 us (6%)
    pallas_call x1, Pallas kernels, shards(): pl.pallas_call(functools.partial(kernel, n, nf, heads), out_shape=pltpu.V...  21.5 us
    unnamed x1, local copies, waits for them, and re-layouts  1.32 us

profile of v3, /device:TPU:0, one launch (start us, length us, event | category | flops | bytes accessed | tf_op | source)
XLA Modules:
  0.0 22.9 jit_solution(8207156491167012879)
XLA Ops:
  0.0 21.5 %shard_map.64 = f32[512,1024]{1,0:T(8,128)S(1)} custom-call(f32[48,2,1024]{2,1,0:T(2,128)} %x_hbm.1, s32[384]{0:T(512)} %det_hbm.1, f32[3,3]{1,0:T(4,128)} %inter_hbm.1, s32[12]{0:T(128)} %lag_hbm.1, s32[2,512]{1,0:T(2,128)} %bitcast.1, bf16[16,224,128]{2,1,0:T(8,128)(2,1)} %constant.2.clone.bess_hbm), custom_call_target="tpu_custom_call" | custom-call | tf_op jit(solution)/shard_map/pallas_call | solution.py:360
  21.6 1.3 %copy.8 = f32[512,1024]{1,0:T(8,128)} copy(f32[512,1024]{1,0:T(8,128)S(1)} %shard_map.64) | data formatting | bytes 4194304

commit v4 on v3

--- a/solution.py
+++ b/solution.py
@@ -288,13 +288,13 @@
                     white[c, h, here, :] = buf[p, g, c, h].astype(jnp.float32)
                     near_rows[c, h, here, :] = buf[p, g, c, h]
 
-        for group in range(0, nlag, 1):
+        for group in range(0, nlag, 2):
             if group == 2:
                 @pl.when(p + 1 < pieces)
                 def _():
                     forward(p + 1)
 
-            slots = range(group, group + 1)
+            slots = range(group, group + 2)
             sums = [[0.0, 0.0] for _ in slots]
             for first, last in [(lo, min(lo + 256, rows)) for lo in range(0, rows, 256)]:
                 count = last - first

time: 23 us -> 23.1 us (level)
  no operation moved by 1% of the time
where the time goes in v4:
time: 23.1 us; the launch traced here: 23 us
  Pallas kernels  21.7 us (94%)
  local copies, waits for them, and re-layouts  1.32 us (6%)
    pallas_call x1, Pallas kernels, shards(): pl.pallas_call(functools.partial(kernel, n, nf, heads), out_shape=pltpu.V...  21.7 us
    unnamed x1, local copies, waits for them, and re-layouts  1.32 us

profile of v4, /device:TPU:0, one launch (start us, length us, event | category | flops | bytes accessed | tf_op | source)
XLA Modules:
  0.0 23.0 jit_solution(5801471909645685036)
XLA Ops:
  0.0 21.7 %shard_map.64 = f32[512,1024]{1,0:T(8,128)S(1)} custom-call(f32[48,2,1024]{2,1,0:T(2,128)} %x_hbm.1, s32[384]{0:T(512)} %det_hbm.1, f32[3,3]{1,0:T(4,128)} %inter_hbm.1, s32[12]{0:T(128)} %lag_hbm.1, s32[2,512]{1,0:T(2,128)} %bitcast.1, bf16[16,224,128]{2,1,0:T(8,128)(2,1)} %constant.2.clone.bess_hbm), custom_call_target="tpu_custom_call" | custom-call | tf_op jit(solution)/shard_map/pallas_call | solution.py:360
  21.7 1.3 %copy.8 = f32[512,1024]{1,0:T(8,128)} copy(f32[512,1024]{1,0:T(8,128)S(1)} %shard_map.64) | data formatting | bytes 4194304
